TPU v7x, 256 devices: a whole 4x4x8 slice. The times are simulated.
256 devices in a mesh: leaf: 64 (over z, y, core), front: 4 (over x).
Axes of the slice: x: 4, y: 4, z: 8, core: 2. Of those that a mesh axis runs over, the one named last changes fastest.
Arguments:
- rhs_leaf: float32 [32, 65536], P(None, ('leaf', 'front')), may hold values from -6 to 6
- rhs_sep: float32 [32, 32768], P(None, ('leaf', 'front')), may hold values from -6 to 6
- inv_leaf: float32 [64, 1024, 1024], P('leaf', 'front'), may hold values from -0.1875 to 0.1875
- inv_sep: float32 [64, 512, 512], P('leaf', 'front'), may hold values from -0.25 to 0.25
- push_leaf: float32 [64, 128, 1024], P('leaf', None, 'front'), may hold values from -0.09375 to 0.09375
- push_sep: float32 [64, 128, 512], P('leaf', None, 'front'), may hold values from -0.125 to 0.125
- pull_leaf: float32 [64, 1024, 128], P('leaf', 'front'), may hold values from -0.25 to 0.25
- pull_sep: float32 [64, 512, 128], P('leaf', 'front'), may hold values from -0.25 to 0.25
- rows_leaf: int32 [64, 128], P('leaf'), may hold values from 0 to 511, as said below
- rows_sep: int32 [64, 128], P('leaf'), may hold values from 0 to 511, as said below
- pivot_leaf: int32 [64, 1024], P('leaf'), may hold values from 0 to 1023, each once within a row
- pivot_sep: int32 [64, 512], P('leaf'), may hold values from 0 to 511, each once within a row
- basis_leaf: float32 [50, 65536], P(None, ('leaf', 'front')), may hold values from -6 to 6
- basis_sep: float32 [50, 32768], P(None, ('leaf', 'front')), may hold values from -6 to 6
Outputs:
- q_leaf: float32 [32, 65536], P(None, ('leaf', 'front'))
- q_sep: float32 [32, 32768], P(None, ('leaf', 'front'))
- coeffs: float32 [50, 32], replicated
- rfac: float32 [32, 32], replicated
Inputs may be any that keep to these rules, and one draw needn't show every extreme that they name: `rows_leaf`: each row holds 128 different rows of a separator front. `rows_sep`: each row holds 128 different rows of a separator front. `pivot_leaf`: each row is a permutation. `pivot_sep`: each row is a permutation.
All inputs are finite; a program needn't handle non-finite values.
Results may differ from a plain program's by a relative error of at most 0.0001.
Values sent between devices are 32-bit elements; how exact they have to be, the bound alone decides.
A program may use at most 64 MiB of HBM per device.

v0:
```python
import functools
import jax
import jax.numpy as jnp
from jax import lax
from jax.sharding import Mesh
from jax.sharding import PartitionSpec as P

LEAF = ("leaf_0", "leaf_1", "leaf_2")
LEAF_FRONT = ("leaf_0", "leaf_1", "leaf_2", "front")
exact_mode = lax.Precision.HIGHEST


def cut_along(array, dim, length):
    lengths = array.shape
    pieces = array.reshape(*lengths[:dim], length, lengths[dim] // length, *lengths[dim + 1 :])
    return jnp.moveaxis(pieces, dim, 0)


def sum_at_owner(array, axis, dim):
    pieces = cut_along(array, dim, lax.axis_size(axis))
    arrived = lax.all_to_all(pieces, axis, split_axis=0, concat_axis=0, tiled=True)
    return arrived.sum(axis=0)


def joined_along(pieces, dim):
    pieces = jnp.moveaxis(pieces, 0, dim)
    lengths = pieces.shape
    return pieces.reshape(*lengths[:dim], lengths[dim] * lengths[dim + 1], *lengths[dim + 2 :])


def from_everyone(array, axis):
    copies = jnp.broadcast_to(array, (lax.axis_size(axis), *array.shape))
    return lax.all_to_all(copies, axis, split_axis=0, concat_axis=0, tiled=True)


def gathered_copies(array, axis, dim):
    return joined_along(from_everyone(array, axis), dim)


def rows_first(arrays, axis, dims):
    turned = [jnp.moveaxis(a, dim, 0) for a, dim in zip(arrays, dims)]
    widths = [t[0].size for t in turned]
    both = jnp.concatenate([t.reshape(-1, w) for t, w in zip(turned, widths)], axis=1)
    whole = lax.all_gather(both, axis, axis=0, tiled=True)
    pieces = jnp.split(whole, [sum(widths[:k]) for k in range(1, len(widths))], axis=1)
    return tuple(
        (
            jnp.moveaxis(b.reshape(-1, *t.shape[1:]), 0, dim)
            for b, t, dim in zip(pieces, turned, dims)
        )
    )


def by_axis(array, axes):
    return functools.reduce(lax.psum, axes, array)


def contract(former, latter):
    return lax.dot_general(
        former,
        latter,
        (((1,), (1,)), ((), ())),
        precision=exact_mode,
        preferred_element_type=jnp.float32,
    )


def expand(coeff_block, basis):
    return jnp.dot(coeff_block.T, basis, precision=exact_mode, preferred_element_type=jnp.float32)


def apply_inverse(gathered, inverse, pivots):
    return contract(gathered[:, pivots], inverse)


def solve_if(active, gathered, inverse, pivots):

    def chosen(operand):
        return apply_inverse(operand, inverse, pivots)

    def skipped(operand):
        return jnp.zeros((operand.shape[0], inverse.shape[0]), jnp.float32)

    return lax.cond(active, chosen, skipped, gathered)


def pick_piece(pool, index, valid):
    safe = jnp.clip(index, 0, pool.shape[0] - 1)
    piece = lax.dynamic_index_in_dim(pool, safe, 0, keepdims=False)
    return jnp.where(valid, piece, jnp.zeros_like(piece))


def push_compact(state, weights):
    return sum_at_owner(contract(state, weights), "front", 1)


def sep_gathered(shares):
    return gathered_copies(shares, "front", 1)


def leaf_gathered(shares):
    return gathered_copies(shares, "front", 1)


def on_device(
    rhs_leaf,
    rhs_sep,
    inv_leaf,
    inv_sep,
    push_leaf,
    push_sep,
    pull_leaf,
    pull_sep,
    rows_leaf,
    rows_sep,
    pivot_leaf,
    pivot_sep,
    basis_leaf,
    basis_sep,
):
    holder = lax.axis_index(LEAF)
    groups = lax.axis_size(LEAF)
    top_level = groups.bit_length() - 1
    sep_width = pivot_sep.shape[1]
    share_width = rhs_sep.shape[1]
    leaf_inverse = inv_leaf[0]
    sep_inverse = inv_sep[0]
    leaf_pivots = pivot_leaf[0]
    sep_pivots = pivot_sep[0]
    level_of = jnp.full((), top_level + 1, jnp.int32)
    for bit_index in range(top_level, 0, -1):
        level_of = jnp.where(holder % 2**bit_index != 0, jnp.int32(bit_index), level_of)
    leaf_state = apply_inverse(leaf_gathered(rhs_leaf), leaf_inverse, leaf_pivots)
    sep_state = jnp.zeros_like(rhs_sep)
    leaf_compact = push_compact(leaf_state, push_leaf[0])
    sep_compact = jnp.zeros_like(leaf_compact)
    front_start = lax.axis_index("front") * share_width
    for height in range(1, top_level + 2):
        if height == 1:
            lower_index = holder - 1
            upper_index = holder
        else:
            lower_index = holder - 2 ** (height - 2)
            upper_index = holder + 2 ** (height - 2)
        lower_valid = jnp.logical_and(lower_index >= 0, height <= top_level)
        upper_valid = upper_index < groups
        source = leaf_compact if height == 1 else sep_compact
        source_rows = rows_leaf[0] if height == 1 else rows_sep[0]
        pool, pool_rows = (
            gathered_copies(source[None], LEAF, 0),
            gathered_copies(source_rows[None], LEAF, 0),
        )
        first_part = pick_piece(pool, upper_index, upper_valid)
        first_rows = pick_piece(pool_rows, upper_index, upper_valid)
        second_part = pick_piece(pool, lower_index, lower_valid)
        second_rows = pick_piece(pool_rows, lower_index, lower_valid)
        first_full, second_full = rows_first((first_part, second_part), "front", (1, 1))
        dense = jnp.zeros((rhs_sep.shape[0], sep_width), jnp.float32)
        dense = dense.at[:, first_rows].add(first_full).at[:, second_rows].add(second_full)
        arriving = lax.dynamic_slice_in_dim(dense, front_start, share_width, 1)
        active = level_of == height
        applied = solve_if(active, sep_gathered(rhs_sep - arriving), sep_inverse, sep_pivots)
        sep_state = jnp.where(active, applied, sep_state)
        if height <= top_level:
            sep_compact = jnp.where(active, push_compact(sep_state, push_sep[0]), sep_compact)
    sep_solution = sep_state
    leaf_solution = leaf_state
    for height in range(top_level, -1, -1):
        if height == top_level:
            parent_index = jnp.zeros((), jnp.int32)
        elif height >= 1:
            parent_index = (2 * (holder // 2 ** (height + 1)) + 1) * 2**height
        else:
            parent_index = holder // 2 * 2 + 1
        pool = gathered_copies(sep_solution[None], LEAF, 0)
        picked = lax.dynamic_index_in_dim(pool, parent_index, 0, keepdims=False)
        parent = gathered_copies(picked, "front", 1)
        if height >= 1:
            lifted = contract(parent[:, rows_sep[0]], pull_sep[0])
            active = level_of == height
            applied = solve_if(active, sep_gathered(lifted), sep_inverse, sep_pivots)
            sep_solution = jnp.where(active, sep_state - applied, sep_solution)
        else:
            lifted = contract(parent[:, rows_leaf[0]], pull_leaf[0])
            leaf_solution = leaf_state - apply_inverse(
                leaf_gathered(lifted), leaf_inverse, leaf_pivots
            )
    total_rows = groups * (pivot_leaf.shape[1] + sep_width)
    first_sum, metric_sum = (
        by_axis(
            contract(basis_leaf, leaf_solution) + contract(basis_sep, sep_solution), LEAF_FRONT
        ),
        by_axis(contract(basis_leaf, basis_leaf) + contract(basis_sep, basis_sep), LEAF_FRONT),
    )
    first_proj = first_sum / total_rows
    metric = metric_sum / total_rows
    once_leaf = leaf_solution - expand(first_proj, basis_leaf)
    once_sep = sep_solution - expand(first_proj, basis_sep)
    second_sum, self_sum = (
        by_axis(contract(basis_leaf, once_leaf) + contract(basis_sep, once_sep), LEAF_FRONT),
        by_axis(contract(once_leaf, once_leaf) + contract(once_sep, once_sep), LEAF_FRONT),
    )
    second = second_sum / total_rows
    twice_leaf = once_leaf - expand(second, basis_leaf)
    twice_sep = once_sep - expand(second, basis_sep)
    cross = jnp.dot(second.T, second, precision=exact_mode, preferred_element_type=jnp.float32)
    curved = jnp.dot(
        second.T,
        jnp.dot(metric, second, precision=exact_mode, preferred_element_type=jnp.float32),
        precision=exact_mode,
        preferred_element_type=jnp.float32,
    )
    gram_matrix = self_sum / total_rows - 2.0 * cross + curved
    lower_factor = jnp.linalg.cholesky(gram_matrix)
    q_leaf = lax.linalg.triangular_solve(lower_factor, twice_leaf, left_side=True, lower=True)
    q_sep = lax.linalg.triangular_solve(lower_factor, twice_sep, left_side=True, lower=True)
    return (q_leaf, q_sep, first_proj + second, lower_factor.T)


def solution(mesh):
    torus = Mesh(
        mesh.devices.reshape(8, 4, 2, mesh.shape["front"]), ("leaf_0", "leaf_1", "leaf_2", "front")
    )
    return jax.shard_map(
        on_device,
        mesh=torus,
        in_specs=(
            P(None, LEAF_FRONT),
            P(None, LEAF_FRONT),
            P(LEAF, "front", None),
            P(LEAF, "front", None),
            P(LEAF, None, "front"),
            P(LEAF, None, "front"),
            P(LEAF, "front", None),
            P(LEAF, "front", None),
            P(LEAF, None),
            P(LEAF, None),
            P(LEAF, None),
            P(LEAF, None),
            P(None, LEAF_FRONT),
            P(None, LEAF_FRONT),
        ),
        out_specs=(P(None, LEAF_FRONT), P(None, LEAF_FRONT), P(), P()),
        check_vma=False,
    )
```

profile of v0, /device:TPU:8, one launch (start us, length us, event | category | flops | bytes accessed | tf_op | source)
XLA Modules:
  0.0 963.4 jit_solution(1290878768696683510)
XLA Ops:
  26.1 12.1 %all-to-all-start.2 = ((s32[64,1,128]{2,1,0:T(1,128)}), s32[64,1,128]{2,1,0:T(1,128)S(1)}, u32[]{:S(2)}, u32[]{:S(2)}) async-start(s32[64,1,128]{2,1,0:T(1,128)} %broadcast_in_dim.199), calls=%async_computation.2 | async-start | bytes 65536 | tf_op jit(solution)/shard_map/all_to_all | solution.py:33
  52.3 12.3 %all-to-all-done.4 = f32[64,1,1024]{2,1,0:T(1,128)S(1)} async-done(((f32[64,1,1024]{2,1,0:T(1,128)}), f32[64,1,1024]{2,1,0:T(1,128)S(1)}, u32[]{:S(2)}, u32[]{:S(2)}) %all-to-all-start.4) | async-done | bytes 262176 | tf_op jit(solution)/shard_map/all_to_all | solution.py:33
  121.8 12.2 %all-to-all-done.7 = f32[64,1,1024]{2,1,0:T(1,128)S(1)} async-done(((f32[64,1,1024]{2,1,0:T(1,128)}), f32[64,1,1024]{2,1,0:T(1,128)S(1)}, u32[]{:S(2)}, u32[]{:S(2)}) %all-to-all-start.7) | async-done | bytes 262176 | tf_op jit(solution)/shard_map/all_to_all | solution.py:33
  135.7 12.1 %all_gather.22 = f32[128,64]{1,0:T(8,128)S(1)} all-gather(f32[32,64]{1,0:T(8,128)S(1)} %pad_maximum_fusion.1), channel_id=1, replica_groups=mesh['leaf_0'=8,'leaf_1'=4,'leaf_2'=2,'front'=4] {'front'}, dimensions={0}, use_global_device_ids=true | all-gather | bytes 40960 | tf_op jit(solution)/shard_map/all_gather | solution.py:44
  171.4 17.6 %all_to_all.233 = f32[64,1,1024]{2,1,0:T(1,128)S(1)} all-to-all(f32[64,1,1024]{2,1,0:T(1,128)S(1)} %reshape.976), channel_id=1, replica_groups=mesh['leaf_0'=8,'leaf_1'=4,'leaf_2'=2,'front'=4] {'leaf_0','leaf_1','lea..., dimensions={0} | all-to-all | bytes 524288 | tf_op jit(solution)/shard_map/all_to_all | solution.py:33
  224.5 19.4 %all_to_all.235 = f32[64,1,1024]{2,1,0:T(1,128)S(1)} all-to-all(f32[64,1,1024]{2,1,0:T(1,128)S(1)} %reshape.980), channel_id=1, replica_groups=mesh['leaf_0'=8,'leaf_1'=4,'leaf_2'=2,'front'=4] {'leaf_0','leaf_1','lea..., dimensions={0} | all-to-all | bytes 524288 | tf_op jit(solution)/shard_map/all_to_all | solution.py:33
  287.3 12.2 %all-to-all-done.16 = f32[64,1,1024]{2,1,0:T(1,128)S(1)} async-done(((f32[64,1,1024]{2,1,0:T(1,128)}), f32[64,1,1024]{2,1,0:T(1,128)S(1)}, u32[]{:S(2)}, u32[]{:S(2)}) %all-to-all-start.16) | async-done | bytes 262176 | tf_op jit(solution)/shard_map/all_to_all | solution.py:33
  301.1 11.9 %all_gather.25 = f32[128,64]{1,0:T(8,128)S(1)} all-gather(f32[32,64]{1,0:T(8,128)S(1)} %pad_maximum_fusion.4), channel_id=1, replica_groups=mesh['leaf_0'=8,'leaf_1'=4,'leaf_2'=2,'front'=4] {'front'}, dimensions={0}, use_global_device_ids=true | all-gather | bytes 40960 | tf_op jit(solution)/shard_map/all_gather | solution.py:44
  335.1 18.4 %all_to_all.238 = f32[64,1,1024]{2,1,0:T(1,128)S(1)} all-to-all(f32[64,1,1024]{2,1,0:T(1,128)S(1)} %reshape.988), channel_id=1, replica_groups=mesh['leaf_0'=8,'leaf_1'=4,'leaf_2'=2,'front'=4] {'leaf_0','leaf_1','lea..., dimensions={0} | all-to-all | bytes 524288 | tf_op jit(solution)/shard_map/all_to_all | solution.py:33
  389.1 18.6 %all_to_all.240 = f32[64,1,1024]{2,1,0:T(1,128)S(1)} all-to-all(f32[64,1,1024]{2,1,0:T(1,128)S(1)} %reshape.992), channel_id=1, replica_groups=mesh['leaf_0'=8,'leaf_1'=4,'leaf_2'=2,'front'=4] {'leaf_0','leaf_1','lea..., dimensions={0} | all-to-all | bytes 524288 | tf_op jit(solution)/shard_map/all_to_all | solution.py:33
  409.3 11.9 %all_gather.27 = f32[128,64]{1,0:T(8,128)S(1)} all-gather(f32[32,64]{1,0:T(8,128)S(1)} %concatenate.27), channel_id=1, replica_groups=mesh['leaf_0'=8,'leaf_1'=4,'leaf_2'=2,'front'=4] {'front'}, dimensions={0}, use_global_device_ids=true | all-gather | bytes 40960 | tf_op jit(solution)/shard_map/all_gather | solution.py:44
  441.8 28.9 %all-to-all-done.24 = f32[64,1,32,128]{3,2,1,0:T(8,128)S(1)} async-done(((f32[64,1,32,128]{3,2,1,0:T(8,128)}), f32[64,1,32,128]{3,2,1,0:T(8,128)S(1)}, u32[]{:S(2)}, u32[]{:S(2)}) %all-to-all-start.24) | async-done | bytes 1048608 | tf_op jit(solution)/shard_map/all_to_all | solution.py:33
  498.2 28.7 %all-to-all-done.27 = f32[64,1,32,128]{3,2,1,0:T(8,128)S(1)} async-done(((f32[64,1,32,128]{3,2,1,0:T(8,128)}), f32[64,1,32,128]{3,2,1,0:T(8,128)S(1)}, u32[]{:S(2)}, u32[]{:S(2)}) %all-to-all-start.27) | async-done | bytes 1048608 | tf_op jit(solution)/shard_map/all_to_all | solution.py:33
  553.0 28.8 %all-to-all-done.30 = f32[64,1,32,128]{3,2,1,0:T(8,128)S(1)} async-done(((f32[64,1,32,128]{3,2,1,0:T(8,128)}), f32[64,1,32,128]{3,2,1,0:T(8,128)S(1)}, u32[]{:S(2)}, u32[]{:S(2)}) %all-to-all-start.30) | async-done | bytes 1048608 | tf_op jit(solution)/shard_map/all_to_all | solution.py:33
  608.3 28.8 %all-to-all-done.33 = f32[64,1,32,128]{3,2,1,0:T(8,128)S(1)} async-done(((f32[64,1,32,128]{3,2,1,0:T(8,128)}), f32[64,1,32,128]{3,2,1,0:T(8,128)S(1)}, u32[]{:S(2)}, u32[]{:S(2)}) %all-to-all-start.33) | async-done | bytes 1048608 | tf_op jit(solution)/shard_map/all_to_all | solution.py:33
  663.9 28.8 %all-to-all-done.36 = f32[64,1,32,128]{3,2,1,0:T(8,128)S(1)} async-done(((f32[64,1,32,128]{3,2,1,0:T(8,128)}), f32[64,1,32,128]{3,2,1,0:T(8,128)S(1)}, u32[]{:S(2)}, u32[]{:S(2)}) %all-to-all-start.36) | async-done | bytes 1048608 | tf_op jit(solution)/shard_map/all_to_all | solution.py:33
  719.8 28.8 %all-to-all-done.39 = f32[64,1,32,128]{3,2,1,0:T(8,128)S(1)} async-done(((f32[64,1,32,128]{3,2,1,0:T(8,128)}), f32[64,1,32,128]{3,2,1,0:T(8,128)S(1)}, u32[]{:S(2)}, u32[]{:S(2)}) %all-to-all-start.39) | async-done | bytes 1048608 | tf_op jit(solution)/shard_map/all_to_all | solution.py:33
  774.3 28.5 %all-to-all-done.42 = f32[64,1,32,128]{3,2,1,0:T(8,128)S(1)} async-done(((f32[64,1,32,128]{3,2,1,0:T(8,128)}), f32[64,1,32,128]{3,2,1,0:T(8,128)S(1)}, u32[]{:S(2)}, u32[]{:S(2)}) %all-to-all-start.42) | async-done | bytes 1048608 | tf_op jit(solution)/shard_map/all_to_all | solution.py:33
  827.9 27.5 %psum.112 = f32[50,32]{0,1:T(8,128)S(1)} all-reduce(f32[50,32]{0,1:T(8,128)S(1)} %fusion.2), channel_id=1, replica_groups=mesh['leaf_0'=8,'leaf_1'=4,'leaf_2'=2,'front'=4] {'leaf_0'}, use_global_device_ids=true, to_apply=%region_47.48 | all-reduce | flops 1600 | bytes 12800 | tf_op jit(solution)/shard_map/psum | solution.py:55
  855.5 14.0 %psum.113 = f32[50,32]{0,1:T(8,128)S(1)} all-reduce(f32[50,32]{0,1:T(8,128)S(1)} %psum.112), channel_id=1, replica_groups=mesh['leaf_0'=8,'leaf_1'=4,'leaf_2'=2,'front'=4] {'leaf_1'}, use_global_device_ids=true, to_apply=%region_48.49 | all-reduce | flops 1600 | bytes 12800 | tf_op jit(solution)/shard_map/psum | solution.py:55
  872.8 15.3 %psum.115 = f32[50,32]{0,1:T(8,128)S(1)} all-reduce(f32[50,32]{0,1:T(8,128)S(1)} %psum.114), channel_id=1, replica_groups=mesh['leaf_0'=8,'leaf_1'=4,'leaf_2'=2,'front'=4] {'front'}, use_global_device_ids=true, to_apply=%region_50.51 | all-reduce | flops 1600 | bytes 12800 | tf_op jit(solution)/shard_map/psum | solution.py:55
  889.1 27.6 %all-reduce.1 = (f32[50,32]{0,1:T(8,128)S(1)}, f32[32,32]{0,1:T(8,128)S(1)}, f32[50,50]{1,0:T(8,128)S(1)}) all-reduce(f32[50,32]{0,1:T(8,128)S(1)} %fusion.1, f32[32,32]{0,1:T(8,128)S(1)} %convolution_add_fusion.3, f32[50,50]{1,0:T(8,128)S(1)} %convolution_add_fusion), channel_id=1, replica_groups=mesh['leaf_0'=8,'leaf_1'=4,'leaf_2'=2,'front'=4] {'leaf_0'}, use_global_device_ids=true, to_apply=%region_55.56 | all-reduce | flops 5124 | bytes 40992 | tf_op jit(solution)/shard_map/psum | solution.py:55
  916.6 17.1 %all-reduce.3 = (f32[50,32]{0,1:T(8,128)S(1)}, f32[32,32]{0,1:T(8,128)S(1)}, f32[50,50]{1,0:T(8,128)S(1)}) all-reduce(f32[50,32]{0,1:T(8,128)S(1)} %get-tuple-element.267, f32[32,32]{0,1:T(8,128)S(1)} %get-tuple-element.268, f32[50,50]{1,0:T(8,128)S(1)} %get-tuple-element.269), channel_id=1, replica_groups=mesh['leaf_0'=8,'leaf_1'=4,'leaf_2'=2,'front'=4] {'leaf_1'}, use_global_device_ids=true, to_apply=%region_56.57 | all-reduce | flops 5124 | bytes 40992 | tf_op jit(solution)/shard_map/psum | solution.py:55
  937.4 15.1 %all-reduce.2 = (f32[50,32]{0,1:T(8,128)S(1)}, f32[32,32]{0,1:T(8,128)S(1)}, f32[50,50]{1,0:T(8,128)S(1)}) all-reduce(f32[50,32]{0,1:T(8,128)S(1)} %get-tuple-element.276, f32[32,32]{0,1:T(8,128)S(1)} %get-tuple-element.277, f32[50,50]{1,0:T(8,128)S(1)} %get-tuple-element.278), channel_id=1, replica_groups=mesh['leaf_0'=8,'leaf_1'=4,'leaf_2'=2,'front'=4] {'front'}, use_global_device_ids=true, to_apply=%region_58.59 | all-reduce | flops 5124 | bytes 40992 | tf_op jit(solution)/shard_map/psum | solution.py:55
  (361 shorter events, 487.9 us)
Async XLA Ops:
  2.1 10.4 %all-to-all-start = ((f32[4,32,256]{2,1,0:T(8,128)}), f32[4,32,256]{2,1,0:T(8,128)S(1)}, u32[]{:S(2)}, u32[]{:S(2)}) async-start(f32[4,32,256]{2,1,0:T(8,128)} %broadcast_in_dim.197), calls=%async_computation | async-start | bytes 262144 | tf_op jit(solution)/shard_map/all_to_all | solution.py:33
  26.1 20.7 %all-to-all-start.2 = ((s32[64,1,128]{2,1,0:T(1,128)}), s32[64,1,128]{2,1,0:T(1,128)S(1)}, u32[]{:S(2)}, u32[]{:S(2)}) async-start(s32[64,1,128]{2,1,0:T(1,128)} %broadcast_in_dim.199), calls=%async_computation.2 | async-start | bytes 65536 | tf_op jit(solution)/shard_map/all_to_all | solution.py:33
  46.7 17.8 %all-to-all-start.4 = ((f32[64,1,1024]{2,1,0:T(1,128)}), f32[64,1,1024]{2,1,0:T(1,128)S(1)}, u32[]{:S(2)}, u32[]{:S(2)}) async-start(f32[64,1,1024]{2,1,0:T(1,128)} %reshape.968), calls=%async_computation.4 | async-start | bytes 524288 | tf_op jit(solution)/shard_map/all_to_all | solution.py:33
  82.0 8.9 all-to-all-start.5
  101.9 14.2 %all-to-all-start.1 = ((s32[64,1,128]{2,1,0:T(1,128)}), s32[64,1,128]{2,1,0:T(1,128)S(1)}, u32[]{:S(2)}, u32[]{:S(2)}) async-start(s32[64,1,128]{2,1,0:T(1,128)} %broadcast_in_dim.198), calls=%async_computation.1 | async-start | bytes 65536 | tf_op jit(solution)/shard_map/all_to_all | solution.py:33
  116.2 17.8 %all-to-all-start.7 = ((f32[64,1,1024]{2,1,0:T(1,128)}), f32[64,1,1024]{2,1,0:T(1,128)S(1)}, u32[]{:S(2)}, u32[]{:S(2)}) async-start(f32[64,1,1024]{2,1,0:T(1,128)} %reshape.972), calls=%async_computation.7 | async-start | bytes 524288 | tf_op jit(solution)/shard_map/all_to_all | solution.py:33
  151.0 8.9 all-to-all-start.8
  205.9 8.9 all-to-all-start.11
  261.0 8.9 all-to-all-start.14
  280.6 18.8 %all-to-all-start.16 = ((f32[64,1,1024]{2,1,0:T(1,128)}), f32[64,1,1024]{2,1,0:T(1,128)S(1)}, u32[]{:S(2)}, u32[]{:S(2)}) async-start(f32[64,1,1024]{2,1,0:T(1,128)} %reshape.984), calls=%async_computation.16 | async-start | bytes 524288 | tf_op jit(solution)/shard_map/all_to_all | solution.py:33
  316.5 8.9 all-to-all-start.17
  370.5 8.9 all-to-all-start.20
  424.7 8.9 all-to-all-start.23
  434.7 35.9 %all-to-all-start.24 = ((f32[64,1,32,128]{3,2,1,0:T(8,128)}), f32[64,1,32,128]{3,2,1,0:T(8,128)S(1)}, u32[]{:S(2)}, u32[]{:S(2)}) async-start(f32[64,1,32,128]{3,2,1,0:T(8,128)} %broadcast_in_dim.214), calls=%async_computation.24 | async-start | bytes 2097152 | tf_op jit(solution)/shard_map/all_to_all | solution.py:33
  471.2 8.9 all-to-all-start.25
  482.0 8.9 all-to-all-start.26
  492.0 35.0 %all-to-all-start.27 = ((f32[64,1,32,128]{3,2,1,0:T(8,128)}), f32[64,1,32,128]{3,2,1,0:T(8,128)S(1)}, u32[]{:S(2)}, u32[]{:S(2)}) async-start(f32[64,1,32,128]{3,2,1,0:T(8,128)} %broadcast_in_dim.217), calls=%async_computation.27 | async-start | bytes 2097152 | tf_op jit(solution)/shard_map/all_to_all | solution.py:33
  536.7 8.9 all-to-all-start.29
  546.7 35.0 %all-to-all-start.30 = ((f32[64,1,32,128]{3,2,1,0:T(8,128)}), f32[64,1,32,128]{3,2,1,0:T(8,128)S(1)}, u32[]{:S(2)}, u32[]{:S(2)}) async-start(f32[64,1,32,128]{3,2,1,0:T(8,128)} %broadcast_in_dim.220), calls=%async_computation.30 | async-start | bytes 2097152 | tf_op jit(solution)/shard_map/all_to_all | solution.py:33
  601.4 35.6 %all-to-all-start.33 = ((f32[64,1,32,128]{3,2,1,0:T(8,128)}), f32[64,1,32,128]{3,2,1,0:T(8,128)S(1)}, u32[]{:S(2)}, u32[]{:S(2)}) async-start(f32[64,1,32,128]{3,2,1,0:T(8,128)} %broadcast_in_dim.223), calls=%async_computation.33 | async-start | bytes 2097152 | tf_op jit(solution)/shard_map/all_to_all | solution.py:33
  656.7 36.0 %all-to-all-start.36 = ((f32[64,1,32,128]{3,2,1,0:T(8,128)}), f32[64,1,32,128]{3,2,1,0:T(8,128)S(1)}, u32[]{:S(2)}, u32[]{:S(2)}) async-start(f32[64,1,32,128]{3,2,1,0:T(8,128)} %broadcast_in_dim.226), calls=%async_computation.36 | async-start | bytes 2097152 | tf_op jit(solution)/shard_map/all_to_all | solution.py:33
  714.1 34.4 %all-to-all-start.39 = ((f32[64,1,32,128]{3,2,1,0:T(8,128)}), f32[64,1,32,128]{3,2,1,0:T(8,128)S(1)}, u32[]{:S(2)}, u32[]{:S(2)}) async-start(f32[64,1,32,128]{3,2,1,0:T(8,128)} %broadcast_in_dim.229), calls=%async_computation.39 | async-start | bytes 2097152 | tf_op jit(solution)/shard_map/all_to_all | solution.py:33
  768.2 34.6 %all-to-all-start.42 = ((f32[64,1,32,128]{3,2,1,0:T(8,128)}), f32[64,1,32,128]{3,2,1,0:T(8,128)S(1)}, u32[]{:S(2)}, u32[]{:S(2)}) async-start(f32[64,1,32,128]{3,2,1,0:T(8,128)} %broadcast_in_dim.232), calls=%async_computation.42 | async-start | bytes 2097152 | tf_op jit(solution)/shard_map/all_to_all | solution.py:33
  814.3 9.3 all-to-all-start.44
  (18 other events, 91.4 us)
where the time goes:
time: 976 us; the launch traced here: 963 us
  blocking collectives  375 us (38%)
  waiting for transfers between devices  345 us (35%)
  starting transfers between devices  137 us (14%)
  local copies, waits for them, and re-layouts  50.8 us (5%)
  other arithmetic  40.4 us (4%)
  matrix products  11.6 us (1%)
    all_to_all x29, waiting for transfers between devices, from_everyone(): return lax.all_to_all(copies, axis, split_axis=0, concat_axis=0, tiled=True)  345 us
    all_to_all x29, starting transfers between devices, from_everyone(): return lax.all_to_all(copies, axis, split_axis=0, concat_axis=0, tiled=True)  137 us
    psum x8, blocking collectives, by_axis(): return functools.reduce(lax.psum, axes, array)  123 us
    all_to_all x9, blocking collectives, from_everyone(): return lax.all_to_all(copies, axis, split_axis=0, concat_axis=0, tiled=True)  114 us
    all_gather x7, blocking collectives, rows_first(): whole = lax.all_gather(both, axis, axis=0, tiled=True)  83.2 us
    all_to_all x7, blocking collectives, sum_at_owner(): lax.all_to_all(pieces, axis, split_axis=0, concat_axis=0, tiled=True)  54 us
    broadcast_in_dim x31, local copies, waits for them, and re-layouts, from_everyone(): copies = jnp.broadcast_to(array, (lax.axis_size(axis), *array.shape))  21 us
  transfers between devices with their start and end apart: 29, of which 29 were waited for; matrix products, arithmetic and copies ran while one was open for 1% of the time, Pallas kernels for 0%

commit v1 on v0

--- a/solution.py
+++ b/solution.py
@@ -41,7 +41,9 @@
     turned = [jnp.moveaxis(a, dim, 0) for a, dim in zip(arrays, dims)]
     widths = [t[0].size for t in turned]
     both = jnp.concatenate([t.reshape(-1, w) for t, w in zip(turned, widths)], axis=1)
-    whole = lax.all_gather(both, axis, axis=0, tiled=True)
+    whole = jnp.concatenate(
+        lax.all_to_all(jnp.stack([both] * lax.axis_size(axis)), axis, 0, 0), axis=0
+    )
     pieces = jnp.split(whole, [sum(widths[:k]) for k in range(1, len(widths))], axis=1)
     return tuple(
         (

time: 976 us -> 957 us (0.981)
  blocking collectives: 375 us -> 322 us
  waiting for transfers between devices: 345 us -> 361 us
  starting transfers between devices: 137 us -> 148 us
    all_gather x7 -> x0, blocking collectives: 83.2 us -> none  [rows_first(): whole = lax.all_gather(both, axis, axis=0, tiled=True)]
    all_to_all x0 -> x4, blocking collectives: none -> 31.6 us  [rows_first(): lax.all_to_all(jnp.stack([both] * lax.axis_size(axis)), axis, 0, 0)]
    all_to_all x0 -> x3, waiting for transfers between devices: none -> 16.2 us  [rows_first(): lax.all_to_all(jnp.stack([both] * lax.axis_size(axis)), axis, 0, 0)]
    all_to_all x0 -> x3, starting transfers between devices: none -> 9.79 us  [rows_first(): lax.all_to_all(jnp.stack([both] * lax.axis_size(axis)), axis, 0, 0)]
  transfers between devices with their start and end apart: 29 -> 32, of which waited for: 29 -> 32; matrix products, arithmetic and copies ran while one was open for 1% -> 1% of each run, Pallas kernels for 0% -> 0%
where the time goes in v1:
time: 957 us; the launch traced here: 945 us
  waiting for transfers between devices  361 us (38%)
  blocking collectives  322 us (34%)
  starting transfers between devices  148 us (15%)
  local copies, waits for them, and re-layouts  52.8 us (6%)
  other arithmetic  45.6 us (5%)
  matrix products  11.6 us (1%)
    all_to_all x29, waiting for transfers between devices, from_everyone(): return lax.all_to_all(copies, axis, split_axis=0, concat_axis=0, tiled=True)  345 us
    all_to_all x29, starting transfers between devices, from_everyone(): return lax.all_to_all(copies, axis, split_axis=0, concat_axis=0, tiled=True)  138 us
    psum x8, blocking collectives, by_axis(): return functools.reduce(lax.psum, axes, array)  124 us
    all_to_all x9, blocking collectives, from_everyone(): return lax.all_to_all(copies, axis, split_axis=0, concat_axis=0, tiled=True)  113 us
    all_to_all x7, blocking collectives, sum_at_owner(): lax.all_to_all(pieces, axis, split_axis=0, concat_axis=0, tiled=True)  54 us
    all_to_all x4, blocking collectives, rows_first(): lax.all_to_all(jnp.stack([both] * lax.axis_size(axis)), axis, 0, 0)  31.6 us
    broadcast_in_dim x31, local copies, waits for them, and re-layouts, from_everyone(): copies = jnp.broadcast_to(array, (lax.axis_size(axis), *array.shape))  21 us
  transfers between devices with their start and end apart: 32, of which 32 were waited for; matrix products, arithmetic and copies ran while one was open for 1% of the time, Pallas kernels for 0%

profile of v1, /device:TPU:8, one launch (start us, length us, event | category | flops | bytes accessed | tf_op | source)
XLA Modules:
  0.0 944.7 jit_solution(15925521521169875260)
XLA Ops:
  27.5 12.1 %all-to-all-start.4 = ((f32[64,1,1024]{2,1,0:T(1,128)}), f32[64,1,1024]{2,1,0:T(1,128)S(1)}, u32[]{:S(2)}, u32[]{:S(2)}) async-start(f32[64,1,1024]{2,1,0:T(1,128)} %reshape.1010), calls=%async_computation.4 | async-start | bytes 524288 | tf_op jit(solution)/shard_map/all_to_all | solution.py:33
  39.6 12.2 %all-to-all-done.4 = f32[64,1,1024]{2,1,0:T(1,128)S(1)} async-done(((f32[64,1,1024]{2,1,0:T(1,128)}), f32[64,1,1024]{2,1,0:T(1,128)S(1)}, u32[]{:S(2)}, u32[]{:S(2)}) %all-to-all-start.4) | async-done | bytes 262176 | tf_op jit(solution)/shard_map/all_to_all | solution.py:33
  106.6 12.3 %all-to-all-done.8 = f32[64,1,1024]{2,1,0:T(1,128)S(1)} async-done(((f32[64,1,1024]{2,1,0:T(1,128)}), f32[64,1,1024]{2,1,0:T(1,128)S(1)}, u32[]{:S(2)}, u32[]{:S(2)}) %all-to-all-start.8) | async-done | bytes 262176 | tf_op jit(solution)/shard_map/all_to_all | solution.py:33
  167.1 16.7 %all_to_all.268 = f32[64,1,1024]{2,1,0:T(1,128)S(1)} all-to-all(f32[64,1,1024]{2,1,0:T(1,128)S(1)} %reshape.1022), channel_id=1, replica_groups=mesh['leaf_0'=8,'leaf_1'=4,'leaf_2'=2,'front'=4] {'leaf_0','leaf_1','lea..., dimensions={0} | all-to-all | bytes 524288 | tf_op jit(solution)/shard_map/all_to_all | solution.py:33
  216.2 19.4 %all_to_all.271 = f32[64,1,1024]{2,1,0:T(1,128)S(1)} all-to-all(f32[64,1,1024]{2,1,0:T(1,128)S(1)} %reshape.1028), channel_id=1, replica_groups=mesh['leaf_0'=8,'leaf_1'=4,'leaf_2'=2,'front'=4] {'leaf_0','leaf_1','lea..., dimensions={0} | all-to-all | bytes 524288 | tf_op jit(solution)/shard_map/all_to_all | solution.py:33
  237.4 8.2 all_to_all.272
  275.8 12.2 %all-to-all-done.20 = f32[64,1,1024]{2,1,0:T(1,128)S(1)} async-done(((f32[64,1,1024]{2,1,0:T(1,128)}), f32[64,1,1024]{2,1,0:T(1,128)S(1)}, u32[]{:S(2)}, u32[]{:S(2)}) %all-to-all-start.20) | async-done | bytes 262176 | tf_op jit(solution)/shard_map/all_to_all | solution.py:33
  322.0 18.4 %all_to_all.275 = f32[64,1,1024]{2,1,0:T(1,128)S(1)} all-to-all(f32[64,1,1024]{2,1,0:T(1,128)S(1)} %reshape.1040), channel_id=1, replica_groups=mesh['leaf_0'=8,'leaf_1'=4,'leaf_2'=2,'front'=4] {'leaf_0','leaf_1','lea..., dimensions={0} | all-to-all | bytes 524288 | tf_op jit(solution)/shard_map/all_to_all | solution.py:33
  373.2 18.4 %all_to_all.278 = f32[64,1,1024]{2,1,0:T(1,128)S(1)} all-to-all(f32[64,1,1024]{2,1,0:T(1,128)S(1)} %reshape.1046), channel_id=1, replica_groups=mesh['leaf_0'=8,'leaf_1'=4,'leaf_2'=2,'front'=4] {'leaf_0','leaf_1','lea..., dimensions={0} | all-to-all | bytes 524288 | tf_op jit(solution)/shard_map/all_to_all | solution.py:33
  422.5 28.9 %all-to-all-done.31 = f32[64,1,32,128]{3,2,1,0:T(8,128)S(1)} async-done(((f32[64,1,32,128]{3,2,1,0:T(8,128)}), f32[64,1,32,128]{3,2,1,0:T(8,128)S(1)}, u32[]{:S(2)}, u32[]{:S(2)}) %all-to-all-start.31) | async-done | bytes 1048608 | tf_op jit(solution)/shard_map/all_to_all | solution.py:33
  479.0 28.7 %all-to-all-done.34 = f32[64,1,32,128]{3,2,1,0:T(8,128)S(1)} async-done(((f32[64,1,32,128]{3,2,1,0:T(8,128)}), f32[64,1,32,128]{3,2,1,0:T(8,128)S(1)}, u32[]{:S(2)}, u32[]{:S(2)}) %all-to-all-start.34) | async-done | bytes 1048608 | tf_op jit(solution)/shard_map/all_to_all | solution.py:33
  507.8 8.0 all_to_all.280
  534.0 28.6 %all-to-all-done.37 = f32[64,1,32,128]{3,2,1,0:T(8,128)S(1)} async-done(((f32[64,1,32,128]{3,2,1,0:T(8,128)}), f32[64,1,32,128]{3,2,1,0:T(8,128)S(1)}, u32[]{:S(2)}, u32[]{:S(2)}) %all-to-all-start.37) | async-done | bytes 1048608 | tf_op jit(solution)/shard_map/all_to_all | solution.py:33
  562.7 8.0 all_to_all.281
  589.2 28.8 %all-to-all-done.40 = f32[64,1,32,128]{3,2,1,0:T(8,128)S(1)} async-done(((f32[64,1,32,128]{3,2,1,0:T(8,128)}), f32[64,1,32,128]{3,2,1,0:T(8,128)S(1)}, u32[]{:S(2)}, u32[]{:S(2)}) %all-to-all-start.40) | async-done | bytes 1048608 | tf_op jit(solution)/shard_map/all_to_all | solution.py:33
  644.9 28.8 %all-to-all-done.43 = f32[64,1,32,128]{3,2,1,0:T(8,128)S(1)} async-done(((f32[64,1,32,128]{3,2,1,0:T(8,128)}), f32[64,1,32,128]{3,2,1,0:T(8,128)S(1)}, u32[]{:S(2)}, u32[]{:S(2)}) %all-to-all-start.43) | async-done | bytes 1048608 | tf_op jit(solution)/shard_map/all_to_all | solution.py:33
  700.8 28.8 %all-to-all-done.46 = f32[64,1,32,128]{3,2,1,0:T(8,128)S(1)} async-done(((f32[64,1,32,128]{3,2,1,0:T(8,128)}), f32[64,1,32,128]{3,2,1,0:T(8,128)S(1)}, u32[]{:S(2)}, u32[]{:S(2)}) %all-to-all-start.46) | async-done | bytes 1048608 | tf_op jit(solution)/shard_map/all_to_all | solution.py:33
  755.2 28.5 %all-to-all-done.49 = f32[64,1,32,128]{3,2,1,0:T(8,128)S(1)} async-done(((f32[64,1,32,128]{3,2,1,0:T(8,128)}), f32[64,1,32,128]{3,2,1,0:T(8,128)S(1)}, u32[]{:S(2)}, u32[]{:S(2)}) %all-to-all-start.49) | async-done | bytes 1048608 | tf_op jit(solution)/shard_map/all_to_all | solution.py:33
  808.9 27.5 %psum.112 = f32[50,32]{0,1:T(8,128)S(1)} all-reduce(f32[50,32]{0,1:T(8,128)S(1)} %fusion.2), channel_id=1, replica_groups=mesh['leaf_0'=8,'leaf_1'=4,'leaf_2'=2,'front'=4] {'leaf_0'}, use_global_device_ids=true, to_apply=%region_47.48 | all-reduce | flops 1600 | bytes 12800 | tf_op jit(solution)/shard_map/psum | solution.py:57
  836.4 14.0 %psum.113 = f32[50,32]{0,1:T(8,128)S(1)} all-reduce(f32[50,32]{0,1:T(8,128)S(1)} %psum.112), channel_id=1, replica_groups=mesh['leaf_0'=8,'leaf_1'=4,'leaf_2'=2,'front'=4] {'leaf_1'}, use_global_device_ids=true, to_apply=%region_48.49 | all-reduce | flops 1600 | bytes 12800 | tf_op jit(solution)/shard_map/psum | solution.py:57
  854.0 15.3 %psum.115 = f32[50,32]{0,1:T(8,128)S(1)} all-reduce(f32[50,32]{0,1:T(8,128)S(1)} %psum.114), channel_id=1, replica_groups=mesh['leaf_0'=8,'leaf_1'=4,'leaf_2'=2,'front'=4] {'front'}, use_global_device_ids=true, to_apply=%region_50.51 | all-reduce | flops 1600 | bytes 12800 | tf_op jit(solution)/shard_map/psum | solution.py:57
  870.3 27.6 %all-reduce.1 = (f32[50,32]{0,1:T(8,128)S(1)}, f32[32,32]{0,1:T(8,128)S(1)}, f32[50,50]{1,0:T(8,128)S(1)}) all-reduce(f32[50,32]{0,1:T(8,128)S(1)} %fusion.1, f32[32,32]{0,1:T(8,128)S(1)} %convolution_add_fusion.3, f32[50,50]{1,0:T(8,128)S(1)} %convolution_add_fusion), channel_id=1, replica_groups=mesh['leaf_0'=8,'leaf_1'=4,'leaf_2'=2,'front'=4] {'leaf_0'}, use_global_device_ids=true, to_apply=%region_55.56 | all-reduce | flops 5124 | bytes 40992 | tf_op jit(solution)/shard_map/psum | solution.py:57
  897.9 17.1 %all-reduce.3 = (f32[50,32]{0,1:T(8,128)S(1)}, f32[32,32]{0,1:T(8,128)S(1)}, f32[50,50]{1,0:T(8,128)S(1)}) all-reduce(f32[50,32]{0,1:T(8,128)S(1)} %get-tuple-element.267, f32[32,32]{0,1:T(8,128)S(1)} %get-tuple-element.268, f32[50,50]{1,0:T(8,128)S(1)} %get-tuple-element.269), channel_id=1, replica_groups=mesh['leaf_0'=8,'leaf_1'=4,'leaf_2'=2,'front'=4] {'leaf_1'}, use_global_device_ids=true, to_apply=%region_56.57 | all-reduce | flops 5124 | bytes 40992 | tf_op jit(solution)/shard_map/psum | solution.py:57
  918.6 15.1 %all-reduce.2 = (f32[50,32]{0,1:T(8,128)S(1)}, f32[32,32]{0,1:T(8,128)S(1)}, f32[50,50]{1,0:T(8,128)S(1)}) all-reduce(f32[50,32]{0,1:T(8,128)S(1)} %get-tuple-element.276, f32[32,32]{0,1:T(8,128)S(1)} %get-tuple-element.277, f32[50,50]{1,0:T(8,128)S(1)} %get-tuple-element.278), channel_id=1, replica_groups=mesh['leaf_0'=8,'leaf_1'=4,'leaf_2'=2,'front'=4] {'front'}, use_global_device_ids=true, to_apply=%region_58.59 | all-reduce | flops 5124 | bytes 40992 | tf_op jit(solution)/shard_map/psum | solution.py:57
  (392 shorter events, 482.0 us)
Async XLA Ops:
  2.1 10.4 %all-to-all-start = ((f32[4,32,256]{2,1,0:T(8,128)}), f32[4,32,256]{2,1,0:T(8,128)S(1)}, u32[]{:S(2)}, u32[]{:S(2)}) async-start(f32[4,32,256]{2,1,0:T(8,128)} %broadcast_in_dim.197), calls=%async_computation | async-start | bytes 262144 | tf_op jit(solution)/shard_map/all_to_all | solution.py:33
  27.5 24.3 %all-to-all-start.4 = ((f32[64,1,1024]{2,1,0:T(1,128)}), f32[64,1,1024]{2,1,0:T(1,128)S(1)}, u32[]{:S(2)}, u32[]{:S(2)}) async-start(f32[64,1,1024]{2,1,0:T(1,128)} %reshape.1010), calls=%async_computation.4 | async-start | bytes 524288 | tf_op jit(solution)/shard_map/all_to_all | solution.py:33
  52.4 14.2 %all-to-all-start.2 = ((s32[64,1,128]{2,1,0:T(1,128)}), s32[64,1,128]{2,1,0:T(1,128)S(1)}, u32[]{:S(2)}, u32[]{:S(2)}) async-start(s32[64,1,128]{2,1,0:T(1,128)} %broadcast_in_dim.199), calls=%async_computation.2 | async-start | bytes 65536 | tf_op jit(solution)/shard_map/all_to_all | solution.py:33
  80.0 8.9 all-to-all-start.6
  100.8 18.1 %all-to-all-start.8 = ((f32[64,1,1024]{2,1,0:T(1,128)}), f32[64,1,1024]{2,1,0:T(1,128)S(1)}, u32[]{:S(2)}, u32[]{:S(2)}) async-start(f32[64,1,1024]{2,1,0:T(1,128)} %reshape.1016), calls=%async_computation.8 | async-start | bytes 524288 | tf_op jit(solution)/shard_map/all_to_all | solution.py:33
  119.5 14.5 %all-to-all-start.1 = ((s32[64,1,128]{2,1,0:T(1,128)}), s32[64,1,128]{2,1,0:T(1,128)S(1)}, u32[]{:S(2)}, u32[]{:S(2)}) async-start(s32[64,1,128]{2,1,0:T(1,128)} %broadcast_in_dim.198), calls=%async_computation.1 | async-start | bytes 65536 | tf_op jit(solution)/shard_map/all_to_all | solution.py:33
  146.8 8.9 all-to-all-start.10
  197.6 8.9 all-to-all-start.14
  249.9 8.9 all-to-all-start.18
  269.2 18.8 %all-to-all-start.20 = ((f32[64,1,1024]{2,1,0:T(1,128)}), f32[64,1,1024]{2,1,0:T(1,128)S(1)}, u32[]{:S(2)}, u32[]{:S(2)}) async-start(f32[64,1,1024]{2,1,0:T(1,128)} %reshape.1034), calls=%async_computation.20 | async-start | bytes 524288 | tf_op jit(solution)/shard_map/all_to_all | solution.py:33
  303.4 8.9 all-to-all-start.22
  354.6 8.9 all-to-all-start.26
  405.5 8.9 all-to-all-start.30
  415.5 35.9 %all-to-all-start.31 = ((f32[64,1,32,128]{3,2,1,0:T(8,128)}), f32[64,1,32,128]{3,2,1,0:T(8,128)S(1)}, u32[]{:S(2)}, u32[]{:S(2)}) async-start(f32[64,1,32,128]{3,2,1,0:T(8,128)} %broadcast_in_dim.214), calls=%async_computation.31 | async-start | bytes 2097152 | tf_op jit(solution)/shard_map/all_to_all | solution.py:33
  452.0 8.9 all-to-all-start.32
  462.7 8.9 all-to-all-start.33
  472.8 35.0 %all-to-all-start.34 = ((f32[64,1,32,128]{3,2,1,0:T(8,128)}), f32[64,1,32,128]{3,2,1,0:T(8,128)S(1)}, u32[]{:S(2)}, u32[]{:S(2)}) async-start(f32[64,1,32,128]{3,2,1,0:T(8,128)} %broadcast_in_dim.217), calls=%async_computation.34 | async-start | bytes 2097152 | tf_op jit(solution)/shard_map/all_to_all | solution.py:33
  517.4 8.9 all-to-all-start.36
  527.4 35.2 %all-to-all-start.37 = ((f32[64,1,32,128]{3,2,1,0:T(8,128)}), f32[64,1,32,128]{3,2,1,0:T(8,128)S(1)}, u32[]{:S(2)}, u32[]{:S(2)}) async-start(f32[64,1,32,128]{3,2,1,0:T(8,128)} %broadcast_in_dim.220), calls=%async_computation.37 | async-start | bytes 2097152 | tf_op jit(solution)/shard_map/all_to_all | solution.py:33
  582.3 35.6 %all-to-all-start.40 = ((f32[64,1,32,128]{3,2,1,0:T(8,128)}), f32[64,1,32,128]{3,2,1,0:T(8,128)S(1)}, u32[]{:S(2)}, u32[]{:S(2)}) async-start(f32[64,1,32,128]{3,2,1,0:T(8,128)} %broadcast_in_dim.223), calls=%async_computation.40 | async-start | bytes 2097152 | tf_op jit(solution)/shard_map/all_to_all | solution.py:33
  637.7 36.0 %all-to-all-start.43 = ((f32[64,1,32,128]{3,2,1,0:T(8,128)}), f32[64,1,32,128]{3,2,1,0:T(8,128)S(1)}, u32[]{:S(2)}, u32[]{:S(2)}) async-start(f32[64,1,32,128]{3,2,1,0:T(8,128)} %broadcast_in_dim.226), calls=%async_computation.43 | async-start | bytes 2097152 | tf_op jit(solution)/shard_map/all_to_all | solution.py:33
  695.1 34.4 %all-to-all-start.46 = ((f32[64,1,32,128]{3,2,1,0:T(8,128)}), f32[64,1,32,128]{3,2,1,0:T(8,128)S(1)}, u32[]{:S(2)}, u32[]{:S(2)}) async-start(f32[64,1,32,128]{3,2,1,0:T(8,128)} %broadcast_in_dim.229), calls=%async_computation.46 | async-start | bytes 2097152 | tf_op jit(solution)/shard_map/all_to_all | solution.py:33
  749.2 34.6 %all-to-all-start.49 = ((f32[64,1,32,128]{3,2,1,0:T(8,128)}), f32[64,1,32,128]{3,2,1,0:T(8,128)S(1)}, u32[]{:S(2)}, u32[]{:S(2)}) async-start(f32[64,1,32,128]{3,2,1,0:T(8,128)} %broadcast_in_dim.232), calls=%async_computation.49 | async-start | bytes 2097152 | tf_op jit(solution)/shard_map/all_to_all | solution.py:33
  795.3 9.3 all-to-all-start.51
  (21 other events, 140.6 us)
